TPU v7x, 256 devices: a whole 4x4x8 slice. The times are simulated.
256 devices in a mesh: grp: 4 (over z_lo), mem: 64 (over x, z_hi, y, core).
Axes of the slice: x: 4, y: 4, z: 8 (z_hi: 2, z_lo: 4; z = z_hi * 4 + z_lo), core: 2. Of those that a mesh axis runs over, the one named last changes fastest.
Arguments:
- embeddings: bfloat16 [262144, 4096], P(('grp', 'mem')), may hold values from -6 to 6
- local_picks: int32 [4, 512], P('grp', 'mem'), may hold values from 0 to 1023
- second_picks: int32 [4, 16], P('grp'), may hold values from 0 to 511
- final_picks: int32 [16], replicated, may hold values from 0 to 63
Outputs:
- gain_table: float32 [64, 512], P('grp', 'mem')
- final_cover: float32 [262144], P(('grp', 'mem'))
Inputs may be any that keep to these rules, and one draw needn't show every extreme that they name: `local_picks`: entry (g, m * 8 + k) names a row among the 1024 points of device m of group g; repeats may occur. `second_picks`: candidate indices of the group, in greedy order; repeats may occur. `final_picks`: index g * 16 + t names group g's second-round pick t; repeats may occur.
All inputs are finite; a program needn't handle non-finite values.
Results may differ from a plain program's by a relative error of at most 0.0003.
Values may be sent and summed in bfloat16 or wider, within the bound.
A program may use at most 64 MiB of HBM per device.

v0:
```python
import jax
import jax.numpy as jnp
from jax import lax
from jax.sharding import PartitionSpec as P

D = 4096


def split_up(x, dim, size):
    before, after = (x.shape[:dim], x.shape[dim + 1 :])
    return jnp.moveaxis(x.reshape(*before, size, -1, *after), dim, 0)


def sent_and_summed(x, axis, dim):
    parts = split_up(x, dim, lax.axis_size(axis))
    arrived = lax.all_to_all(parts, axis, split_axis=0, concat_axis=0, tiled=True)
    return arrived.sum(axis=0)


def per_device(embeddings, local_picks, second_picks, final_picks):
    scaling = float(D) ** (-0.5)
    point_count = embeddings.shape[0]
    local_count = local_picks.shape[1]
    second_list = second_picks[0]
    rounds = second_list.shape[0]
    member = lax.axis_index("mem")
    choose = (local_picks[0][:, None] == lax.iota(jnp.int32, point_count)[None, :]).astype(
        jnp.bfloat16
    )
    own_rows = jnp.dot(choose, embeddings, preferred_element_type=jnp.float32).astype(jnp.bfloat16)

    def similar(other_rows):
        dims = (((1,), (1,)), ((), ()))
        return (
            lax.dot_general(embeddings, other_rows, dims, preferred_element_type=jnp.float32)
            * scaling
        )

    similar_map = similar(lax.all_gather(own_rows, "mem", axis=0, tiled=True))
    group_index = lax.axis_index("grp")
    wanted_group = final_picks // rounds
    winner_slot = final_picks % rounds
    cand_index = jnp.take(second_list, winner_slot)
    owned = (wanted_group == group_index) & (cand_index // local_count == member)
    local_slot = cand_index - member * local_count
    select_table = (
        (local_slot[:, None] == lax.iota(jnp.int32, local_count)[None, :]) & owned[:, None]
    ).astype(jnp.bfloat16)
    row_terms = jnp.dot(select_table, own_rows, preferred_element_type=jnp.float32)
    final_rows = lax.psum(row_terms, ("grp", "mem")).astype(jnp.bfloat16)
    own_block = lax.dynamic_slice_in_dim(similar_map, member * local_count, local_count, 1)
    coverage = jnp.max(own_block, axis=1)
    chosen_cols = jnp.take(similar_map, second_list, axis=1)

    def greedy_step(cover_now, column):
        partial_value = jnp.sum(jnp.maximum(similar_map - cover_now[:, None], 0.0), axis=0)
        return (jnp.maximum(cover_now, column), partial_value)

    _, partials = lax.scan(greedy_step, coverage, chosen_cols.T)
    gain_table = sent_and_summed(partials, "mem", 1) / point_count
    final_cover = jnp.max(similar(final_rows), axis=1)
    return (gain_table, final_cover)


def solution(mesh):
    placed = (P(("grp", "mem"), None), P("grp", "mem"), P("grp", None), P())
    return jax.shard_map(
        per_device,
        mesh=mesh,
        in_specs=placed,
        out_specs=(P("grp", "mem"), P(("grp", "mem"))),
        check_vma=False,
    )
```

profile of v0, /device:TPU:1, one launch (start us, length us, event | category | flops | bytes accessed | tf_op | source)
XLA Modules:
  0.0 156.5 jit_solution(1627441644940368098)
XLA Ops:
  7.2 0.0 all-gather.2.cloned.1.call-start
  7.2 0.0 copy-start.2
  7.2 0.0 copy-start
  7.2 5.3 %convolution_convert_fusion = bf16[8,4096]{1,0:T(8,128)(2,1)} fusion(bf16[1024,4096]{1,0:T(8,128)(2,1)} %param.6, s32[8]{0:T(128)} %bitcast.33), kind=kOutput, calls=%fused_computation.4 | convolution fusion | flops 67149824 | bytes 8454176 | tf_op jit(solution)/shard_map/dot_general | solution.py:30
  12.5 0.0 all-gather.2.cloned.1.call-update
  12.6 0.0 copy-done.2
  12.6 0.0 copy-done
  12.6 0.7 gather_fusion.1
  13.3 1.1 fusion.4
  14.4 85.0 %all-reduce.1 = bf16[16,4096]{1,0:T(8,128)(2,1)S(1)} all-reduce(f32[16,4096]{1,0:T(8,128)S(1)} %fusion.4), channel_id=1, replica_groups=mesh['grp'=4,'mem'=64] {'grp','mem'}, use_global_device_ids=true, to_apply=%region_5.6 | all-reduce | flops 65536 | bytes 393216 | tf_op jit(solution)/shard_map/psum | solution.py:50
  99.5 10.2 %all-gather.2.cloned.1.call-done = bf16[512,4096]{1,0:T(8,128)(2,1)} async-done(((bf16[8,4096]{1,0:T(8,128)(2,1)}), bf16[512,4096]{1,0:T(8,128)(2,1)}) %all-gather.2.cloned.1.call-update) | async-done | bytes 4194320 | tf_op jit(solution)/shard_map/all_gather | solution.py:39
  109.7 8.2 %convolution_multiply_fusion = f32[512,1024]{1,0:T(8,128)S(1)} fusion(bf16[512,4096]{1,0:T(8,128)(2,1)} %all-gather.2.cloned.1.call-done, bf16[1024,4096]{1,0:T(8,128)(2,1)} %param.6), kind=kOutput, calls=%fused_computation.5 | convolution fusion | flops 4295491584 | bytes 14680064 | tf_op jit(solution)/shard_map/dot_general | solution.py:35
  117.9 0.0 copy-start.1
  117.9 1.3 copy-done.1
  119.2 1.9 %copy.7 = f32[1024,512]{1,0:T(8,128)S(1)} copy(f32[1024,512]{0,1:T(8,128)} %bitcast.29) | data formatting | bytes 4194304 | tf_op jit(solution)/shard_map/while | solution.py:59
  121.2 2.2 %gather_fusion = f32[16,1024]{1,0:T(8,128)S(1)} fusion(f32[1024,512]{0,1:T(8,128)} %bitcast.30, s32[1024]{0:T(1024)S(1)} %pad_clamp_fusion.1), kind=kCustom, calls=%fused_computation | custom fusion | bytes 131136 | tf_op jit(solution)/shard_map/jit(_take)/gather | solution.py:53
  123.4 0.1 broadcast_select_fusion
  123.5 6.4 %while.12 = (s32[]{:T(128)}, f32[1024]{0:T(1024)S(1)}, f32[16,512]{1,0:T(8,128)S(1)}, f32[16,1024]{1,0:T(8,128)S(1)}, f32[1024,512]{1,0:T(8,128)S(1)}, /*index=5*/s32[]{:T(128)}, s32[]{:T(128)}) while((s32[]{:T(128)}, f32[1024]{0:T(1024)S(1)}, f32[16,512]{1,0:T(8,128)S(1)}, f32[16,1024]{1,0:T(8,128)S(1)}, f32[1024,512]{1,0:T(8,128)S(1)}, ...), condition=%wide.region_3.4_spmd, body=%wide.region_1.3_spmd.sunk | while | flops 1573378 | bytes 2127965 | solution.py:59
  123.5 0.3 maximum_reduce_fusion.2
  123.8 0.1 dynamic_update_slice.5
  123.9 0.3 maximum_reduce_fusion.2
  124.2 0.1 dynamic_update_slice.5
  124.3 0.3 maximum_reduce_fusion.2
  124.6 0.1 dynamic_update_slice.5
  124.7 0.3 maximum_reduce_fusion.2
  125.0 0.1 dynamic_update_slice.5
  125.1 0.3 maximum_reduce_fusion.2
  125.4 0.1 dynamic_update_slice.5
  125.5 0.3 maximum_reduce_fusion.2
  125.8 0.1 dynamic_update_slice.5
  125.9 0.3 maximum_reduce_fusion.2
  126.2 0.1 dynamic_update_slice.5
  126.3 0.3 maximum_reduce_fusion.2
  126.6 0.1 dynamic_update_slice.5
  126.7 0.3 maximum_reduce_fusion.2
  127.0 0.1 dynamic_update_slice.5
  127.1 0.3 maximum_reduce_fusion.2
  127.4 0.1 dynamic_update_slice.5
  127.5 0.3 maximum_reduce_fusion.2
  127.8 0.1 dynamic_update_slice.5
  127.9 0.3 maximum_reduce_fusion.2
  128.2 0.1 dynamic_update_slice.5
  128.3 0.3 maximum_reduce_fusion.2
  128.6 0.1 dynamic_update_slice.5
  128.7 0.3 maximum_reduce_fusion.2
  129.0 0.1 dynamic_update_slice.5
  129.1 0.3 maximum_reduce_fusion.2
  129.4 0.1 dynamic_update_slice.5
  129.5 0.3 maximum_reduce_fusion.2
  129.8 0.1 dynamic_update_slice.5
  129.9 0.1 copy.8
  130.0 0.8 reshape.71
  130.8 5.1 %all-to-all-start = ((f32[64,1,128]{2,1,0:T(1,128)}), f32[64,1,128]{2,1,0:T(1,128)S(1)}, u32[]{:S(2)}, u32[]{:S(2)}) async-start(f32[64,1,128]{2,1,0:T(1,128)} %reshape.71), calls=%async_computation | async-start | bytes 65536 | tf_op jit(solution)/shard_map/all_to_all | solution.py:16
  135.9 6.3 %fusion = f32[1024]{0:T(1024)} fusion(bf16[1024,4096]{1,0:T(8,128)(2,1)} %param.6, bf16[16,4096]{1,0:T(8,128)(2,1)S(1)} %all-reduce.1), kind=kOutput, calls=%fused_computation.7 | convolution fusion | flops 134249472 | bytes 8523776 | tf_op jit(solution)/shard_map/dot_general | solution.py:35
  142.1 5.5 %all-to-all-done = f32[64,1,128]{2,1,0:T(1,128)S(1)} async-done(((f32[64,1,128]{2,1,0:T(1,128)}), f32[64,1,128]{2,1,0:T(1,128)S(1)}, u32[]{:S(2)}, u32[]{:S(2)}) %all-to-all-start) | async-done | bytes 32800 | tf_op jit(solution)/shard_map/all_to_all | solution.py:16
  147.6 0.5 broadcast.98
  148.1 0.7 reduce.2
  148.8 0.1 reshape.72
  149.0 0.1 bitcast_reduce_fusion
  149.0 0.6 broadcast_multiply_fusion
  (42 shorter events, 0.4 us)
Async XLA Ops:
  7.2 102.5 %all-gather.2.cloned.1.call-start = ((), (), s32[]{:S(2)}) async-start(), calls=%async_computation.1 | async-start | bytes 4259840 | tf_op jit(solution)/shard_map/all_gather | solution.py:39
  7.2 5.3 %copy-start.2 = (s32[16]{0:T(128)S(1)}, s32[16]{0:T(128)}, u32[]{:S(2)}) copy-start(s32[16]{0:T(128)} %param.9) | copy-start | bytes 196
  7.2 5.4 %copy-start = (s32[1,16]{1,0:T(1,128)S(1)}, s32[1,16]{1,0:T(1,128)}, u32[]{:S(2)}) copy-start(s32[1,16]{1,0:T(1,128)} %param.8) | copy-start | bytes 196
  117.9 1.4 copy-start.1
  130.8 16.8 %all-to-all-start = ((f32[64,1,128]{2,1,0:T(1,128)}), f32[64,1,128]{2,1,0:T(1,128)S(1)}, u32[]{:S(2)}, u32[]{:S(2)}) async-start(f32[64,1,128]{2,1,0:T(1,128)} %reshape.71), calls=%async_computation | async-start | bytes 65536 | tf_op jit(solution)/shard_map/all_to_all | solution.py:16
Sparse Core Ops, SparseCore 0:
  12.7 96.9 all-gather.1
where the time goes:
time: 157 us; the launch traced here: 156 us
  blocking collectives  85 us (54%)
  matrix products  20.8 us (13%)
  waiting for transfers between devices  15.7 us (10%)
  between operations  14.2 us (9%)
  local copies, waits for them, and re-layouts  8.8 us (6%)
  other arithmetic  6.21 us (4%)
  starting transfers between devices  5.12 us (3%)
    psum x1, blocking collectives, per_device(): final_rows = lax.psum(row_terms, ('grp', 'mem')).astype(jnp.bfloat16)  85 us
    dot_general x2, matrix products, similar(): lax.dot_general(embeddings, other_rows, dims, preferred_element_type=jnp....  14.5 us
    all_gather x1, waiting for transfers between devices, per_device(): similar_map = similar(lax.all_gather(own_rows, 'mem', axis=0, tiled=True))  10.2 us
    all_to_all x1, waiting for transfers between devices, sent_and_summed(): lax.all_to_all(parts, axis, split_axis=0, concat_axis=0, tiled=True)  5.46 us
    dot_general x1, matrix products, per_device(): jnp.dot(choose, embeddings, preferred_element_type=jnp.float32)  5.28 us
    all_to_all x1, starting transfers between devices, sent_and_summed(): lax.all_to_all(parts, axis, split_axis=0, concat_axis=0, tiled=True)  5.08 us
    reduce_sum x16, other arithmetic, greedy_step(): jnp.sum(jnp.maximum(similar_map - cover_now[:, None], 0.0), axis=0)  4.57 us
  transfers between devices with their start and end apart: 2, of which 2 were waited for; matrix products, arithmetic and copies ran while one was open for 5% of the time, Pallas kernels for 0%

commit v1 on v0

v1 whole, which is shorter than its diff:
```python
import functools

import jax
import jax.numpy as jnp
from jax import lax
from jax.experimental import pallas as pl
from jax.experimental.pallas import tpu as pltpu
from jax.sharding import PartitionSpec as P

MESH = pl.DeviceIdType.MESH
F32 = jnp.float32
BF16 = jnp.bfloat16

D = 4096
P_DEV = 1024
K1 = 8
ROUNDS = 16
FINALS = 16
N_MEM = 64
N_GRP = 4
SIDE = 4
J = 4
KC = D // J
X_PARTS = 8
NT = 256
HALF = J // 2
ORDER = ["l0", "l1", "l2", "l3", "a0", "a1", "a2", "a3", "l4", "l5", "b0", "b1", "l6", "l7"]
ORDER += ["a4", "a5", "b2", "b3", "c0", "c1", "a6", "a7", "c2", "c3", "b4", "b5", "b6", "b7"]
ORDER += ["c4", "c5", "m0", "m1", "c6", "c7", "m2", "m3"]


def kernel(
    local_ref, second_ref, final_ref, x_hbm, gain_ref, cover_ref,
    xs, cand, sim, cov, cov_sum, gains, arrived, f_rows, f_send, f_recv, f_all,
    load_sem, z_send, z_recv, light_send, light_recv, heavy_send, heavy_recv,
    d2d_send, d2d_recv, a2a_send, a2a_recv, fs_send, fs_recv, fd_send, fd_recv,
):
    g = lax.axis_index("grp")
    m = lax.axis_index("mem")
    c = m % 2
    y = (m // 2) % SIDE
    z = (m // 8) % 2
    x = m // 16
    turn = 1 - 2 * c

    def device(xx, zz, yy, cc):
        return (g, ((xx * 2 + zz) * SIDE + yy) * 2 + cc)

    def around(v, step):
        return (v + step + SIDE) % SIDE

    rows8 = P_DEV // 8 // X_PARTS
    loads = [
        pltpu.make_async_copy(
            x_hbm.at[pl.ds(i * rows8, rows8)], xs.at[pl.ds(i * rows8, rows8)], load_sem.at[i]
        )
        for i in range(X_PARTS)
    ]
    for copy in loads:
        copy.start()

    barrier = pltpu.get_barrier_semaphore()
    greeted = [device(around(x, s), z, y, c) for s in (1, 2, 3)]
    greeted += [device(x, z, around(y, s), c) for s in (1, 2, 3)]
    greeted += [device(x, 1 - z, y, c), device(x, z, y, 1 - c)]
    greeted += [((g + s) % N_GRP, m) for s in (1, 2, 3)]
    for other in greeted:
        pl.semaphore_signal(barrier, inc=1, device_id=other, device_id_type=MESH)

    for copy in loads:
        copy.wait()

    sub8 = lax.broadcasted_iota(jnp.int32, (8, D), 0)
    own = jnp.zeros((8, D), F32)
    for k in range(K1):
        r = local_ref[0, k]
        tile = xs[r // 8].astype(F32)
        row = jnp.sum(jnp.where(sub8 == r % 8, tile, 0.0), axis=0, keepdims=True)
        own = jnp.where(sub8 == k, row, own)
    own = own.astype(BF16)
    for j in range(J):
        cand[j, x, z, y, c] = own[:, j * KC : (j + 1) * KC]

    pl.semaphore_wait(barrier, len(greeted))

    def remote(src, send, recv, to):
        return pltpu.make_async_remote_copy(
            src_ref=src, dst_ref=src, send_sem=send, recv_sem=recv, device_id=to, device_id_type=MESH
        )

    def z_copy(j):
        src = cand.at[j, x, z, y, c]
        return remote(src, z_send.at[j], z_recv.at[j], device(x, 1 - z, y, c))

    def plane(i):
        return z if i < J else 1 - z

    def x_first(i):
        return i % 2 == 0

    def light(i, s):
        src = cand.at[i % J, x, plane(i), y, c]
        to = device(around(x, s), z, y, c) if x_first(i) else device(x, z, around(y, s), c)
        return remote(src, light_send.at[i, s - 1], light_recv.at[i, s - 1], to)

    def row_of(i, b, cc):
        if x_first(i):
            return cand.at[i % J, :, plane(i), b, cc]
        return cand.at[i % J, b, plane(i), :, cc]

    def place(i):
        return y if x_first(i) else x

    def beside(i, s):
        if x_first(i):
            return device(x, z, around(y, s), c)
        return device(around(x, s), z, y, c)

    def heavy(i, slot):
        b = place(i)
        if slot == 2:
            src, to = row_of(i, around(b, -turn), c), beside(i, turn)
        else:
            src, to = row_of(i, b, c), beside(i, 1 if slot == 0 else -1)
        return remote(src, heavy_send.at[i, slot], heavy_recv.at[i, slot], to)

    def across(i, step):
        src = row_of(i, around(place(i), step), c)
        return remote(src, d2d_send.at[i, step], d2d_recv.at[i, step], device(x, z, y, 1 - c))

    def stage_l(i):
        if i >= J:
            z_copy(i - J).wait_recv()
        for s in (1, 3, 2):
            light(i, s).start()

    def stage_a(i):
        for s in (1, 2, 3):
            light(i, s).wait_recv()
        heavy(i, 0).start()
        heavy(i, 1).start()
        across(i, 0).start()

    def stage_b(i):
        heavy(i, 0).wait_recv()
        heavy(i, 1).wait_recv()
        heavy(i, 2).start()
        across(i, 1).start()
        across(i, 3).start()

    def stage_c(i):
        heavy(i, 2).wait_recv()
        across(i, 2).start()

    def stage_m(j):
        for i in (j, j + J):
            for step in range(SIDE):
                across(i, step).wait_recv()

        def tile(n, carry):
            at = pl.multiple_of(n * (NT // 8), NT // 8)
            lhs = cand[j].reshape(N_MEM * K1, KC)
            rhs = xs[pl.ds(at, NT // 8), :, j * KC : (j + 1) * KC].reshape(NT, KC)
            part = lax.dot_general(
                lhs, rhs, (((1,), (1,)), ((), ())), preferred_element_type=F32
            ).reshape(N_MEM, K1, NT)
            cols = pl.ds(pl.multiple_of(n * NT, NT), NT)
            if j == 0:
                sim[:, :, cols] = part
            else:
                sim[:, :, cols] += part
            return carry

        lax.fori_loop(0, P_DEV // NT, tile, 0)

    for j in range(J):
        z_copy(j).start()
    stages = {"l": stage_l, "a": stage_a, "b": stage_b, "c": stage_c, "m": stage_m}
    for word in ORDER:
        stages[word[0]](int(word[1:]))

    sub_h = lax.broadcasted_iota(jnp.int32, (8, KC), 0)

    def pick_final(q, carry):
        f = final_ref[q]
        chosen = second_ref[0, f % ROUNDS]
        owner = chosen // K1
        keep = jnp.where(f // ROUNDS == g, chosen % K1, 8)
        for h in range(HALF):
            tile = cand[c * HALF + h, owner // 16, (owner // 8) % 2, (owner // 2) % SIDE, owner % 2]
            row = jnp.sum(jnp.where(sub_h == keep, tile.astype(F32), 0.0), axis=0, keepdims=True)
            f_rows[h, pl.ds(q, 1), :] = row
        return carry

    lax.fori_loop(0, FINALS, pick_final, 0)
    f_send[...] = f_rows[...].astype(BF16)

    cover = jnp.max(sim[m], axis=0, keepdims=True)
    sub_p = lax.broadcasted_iota(jnp.int32, (8, P_DEV), 0)
    for t in range(ROUNDS):
        wide = jnp.broadcast_to(cover, (8, P_DEV))
        cov[t] = wide
        total = wide[:, 0:128]
        for u in range(1, P_DEV // 128):
            total = total + wide[:, u * 128 : (u + 1) * 128]
        cov_sum[t] = total
        chosen = second_ref[0, t]
        tile = jnp.where(sub_p == chosen % K1, sim[chosen // K1], -jnp.inf)
        cover = jnp.maximum(cover, jnp.max(tile, axis=0, keepdims=True))

    def final_copy(s):
        return pltpu.make_async_remote_copy(
            src_ref=f_send, dst_ref=f_recv.at[s - 1], send_sem=fs_send.at[s - 1],
            recv_sem=fs_recv.at[s - 1], device_id=((g + s) % N_GRP, m), device_id_type=MESH,
        )

    for s in (1, 2, 3):
        final_copy(s).start()

    lane = lax.broadcasted_iota(jnp.int32, (8, 128), 1)
    sub = lax.broadcasted_iota(jnp.int32, (8, 128), 0)

    def member_at(e):
        zz = jnp.where(e < 32, 1 - z, z)
        xx = (x + (e // 8) % 4) % SIDE
        yy = (y + (e // 2) % 4) % SIDE
        cc = (c + e + 1) % 2
        return ((xx * 2 + zz) * SIDE + yy) * 2 + cc

    def result_copy(to):
        return pltpu.make_async_remote_copy(
            src_ref=gains.at[to], dst_ref=arrived.at[m], send_sem=a2a_send, recv_sem=a2a_recv,
            device_id=(g, to), device_id_type=MESH,
        )

    def send_pair(i):
        for e in (2 * i, 2 * i + 1):
            to = member_at(e)

            @pl.when(to != m)
            def _():
                result_copy(to).start()

    def gain_pair(i, carry):
        @pl.when(i > 0)
        def _():
            send_pair(i - 1)

        a, b = member_at(2 * i), member_at(2 * i + 1)
        out_a = jnp.zeros((8, 128), F32)
        out_b = jnp.zeros((8, 128), F32)
        tile_a, tile_b = sim[a], sim[b]
        for t in range(ROUNDS):
            sum_a = sum_b = None
            for u in range(P_DEV // 128):
                now = cov[t, :, u * 128 : (u + 1) * 128]
                over_a = jnp.maximum(tile_a[:, u * 128 : (u + 1) * 128], now)
                over_b = jnp.maximum(tile_b[:, u * 128 : (u + 1) * 128], now)
                sum_a = over_a if u == 0 else sum_a + over_a
                sum_b = over_b if u == 0 else sum_b + over_b
            sum_a = jnp.sum(sum_a - cov_sum[t], axis=1, keepdims=True)
            sum_b = jnp.sum(sum_b - cov_sum[t], axis=1, keepdims=True)
            out_a = jnp.where(lane % ROUNDS == t, sum_a, out_a)
            out_b = jnp.where(lane % ROUNDS == t, sum_b, out_b)
        for to, out in ((a, out_a), (b, out_b)):
            gains[to] = jnp.sum(jnp.where(lane // ROUNDS == sub, out, 0.0), axis=0, keepdims=True)
        return carry

    lax.fori_loop(0, N_MEM // 2, gain_pair, 0)
    arrived[m] = gains[m]
    send_pair(N_MEM // 2 - 1)

    for s in (1, 2, 3):
        final_copy(s).wait_recv()
    rows = f_send[...].astype(F32)
    for s in range(3):
        rows = rows + f_recv[s].astype(F32)
    f_all[pl.ds(c * HALF, HALF)] = rows.astype(BF16)
    half_copy = remote(f_all.at[pl.ds(c * HALF, HALF)], fd_send, fd_recv, device(x, z, y, 1 - c))
    half_copy.start()
    half_copy.wait_recv()

    def final_tile(n, carry):
        at = pl.multiple_of(n * (NT // 8), NT // 8)
        part = jnp.zeros((NT, FINALS), F32)
        for j in range(J):
            lhs = xs[pl.ds(at, NT // 8), :, j * KC : (j + 1) * KC].reshape(NT, KC)
            part = part + lax.dot_general(
                lhs, f_all[j], (((1,), (1,)), ((), ())), preferred_element_type=F32
            )
        best = jnp.max(part.T, axis=0, keepdims=True) * (D**-0.5)
        cover_ref[:, pl.ds(pl.multiple_of(n * NT, NT), NT)] = best
        return carry

    lax.fori_loop(0, P_DEV // NT, final_tile, 0)

    several = pl.ds(0, N_MEM - 1)
    pltpu.make_async_copy(arrived.at[several], arrived.at[several], a2a_recv).wait()
    gain_ref[...] = jnp.sum(arrived[...], axis=0) * (D**-0.5 / P_DEV)

    pltpu.make_async_copy(gains.at[several], gains.at[several], a2a_send).wait()
    half_copy.wait_send()
    for s in (1, 2, 3):
        final_copy(s).wait_send()
    for j in range(J):
        z_copy(j).wait_send()
    for i in range(2 * J):
        for s in (1, 2, 3):
            light(i, s).wait_send()
        for slot in range(3):
            heavy(i, slot).wait_send()
        for step in range(SIDE):
            across(i, step).wait_send()


def per_device(embeddings, local_picks, second_picks, final_picks):
    smem = pl.BlockSpec(memory_space=pltpu.SMEM)
    vmem = pl.BlockSpec(memory_space=pltpu.VMEM)
    dma = pltpu.SemaphoreType.DMA
    gain, cover = pl.pallas_call(
        kernel,
        out_shape=(
            jax.ShapeDtypeStruct((1, 128), F32),
            jax.ShapeDtypeStruct((1, P_DEV), F32),
        ),
        in_specs=[smem, smem, smem, pl.BlockSpec(memory_space=pl.ANY)],
        out_specs=(vmem, vmem),
        scratch_shapes=[
            pltpu.VMEM((P_DEV // 8, 8, D), BF16),
            pltpu.VMEM((J, SIDE, 2, SIDE, 2, K1, KC), BF16),
            pltpu.VMEM((N_MEM, K1, P_DEV), F32),
            pltpu.VMEM((ROUNDS, 8, P_DEV), F32),
            pltpu.VMEM((ROUNDS, 8, 128), F32),
            pltpu.VMEM((N_MEM, 1, 128), F32),
            pltpu.VMEM((N_MEM, 1, 128), F32),
            pltpu.VMEM((HALF, FINALS, KC), F32),
            pltpu.VMEM((HALF, FINALS, KC), BF16),
            pltpu.VMEM((3, HALF, FINALS, KC), BF16),
            pltpu.VMEM((J, FINALS, KC), BF16),
            dma((X_PARTS,)),
            dma((J,)),
            dma((J,)),
            dma((2 * J, 3)),
            dma((2 * J, 3)),
            dma((2 * J, 3)),
            dma((2 * J, 3)),
            dma((2 * J, SIDE)),
            dma((2 * J, SIDE)),
            dma,
            dma,
            dma((3,)),
            dma((3,)),
            dma,
            dma,
        ],
        compiler_params=pltpu.CompilerParams(collective_id=0, has_side_effects=True),
        name="coreset",
    )(local_picks, second_picks, final_picks, embeddings.reshape(P_DEV // 8, 8, D))
    return gain.reshape(K1, ROUNDS).T, cover.reshape(P_DEV)


def solution(mesh):
    placed = (P(("grp", "mem"), None), P("grp", "mem"), P("grp", None), P())
    return jax.shard_map(
        per_device,
        mesh=mesh,
        in_specs=placed,
        out_specs=(P("grp", "mem"), P(("grp", "mem"))),
        check_vma=False,
    )
```

time: 157 us -> 59.4 us (0.38)
  blocking collectives: 85 us -> 0 us
  Pallas kernels: 0 us -> 54.9 us
  matrix products: 20.8 us -> 0 us
  waiting for transfers between devices: 15.7 us -> 0 us
  between operations: 14.2 us -> 0.64 us
  local copies, waits for them, and re-layouts: 8.8 us -> 2.46 us
  starting transfers between devices: 5.12 us -> 0 us
  other arithmetic: 6.21 us -> 1.26 us
    psum x1 -> x0, blocking collectives: 85 us -> none  [per_device(): final_rows = lax.psum(row_terms, ('grp', 'mem')).astype(jnp.bfloat16)]
    pallas_call x0 -> x1, Pallas kernels: none -> 54.9 us  [per_device(): pl.pallas_call(kernel, out_shape=(jax.ShapeDtypeStruct((1, 128), F32), ja...]
    dot_general x4 -> x0, matrix products: 20.8 us -> none  [the longest x2 14.5 us: similar(): lax.dot_general(embeddings, other_rows, dims, preferred_element_type=jnp....]
    all_gather x1 -> x0, waiting for transfers between devices: 10.2 us -> none  [per_device(): similar_map = similar(lax.all_gather(own_rows, 'mem', axis=0, tiled=True))]
    all_to_all x1 -> x0, waiting for transfers between devices: 5.46 us -> none  [sent_and_summed(): lax.all_to_all(parts, axis, split_axis=0, concat_axis=0, tiled=True)]
    all_to_all x1 -> x0, starting transfers between devices: 5.08 us -> none  [sent_and_summed(): lax.all_to_all(parts, axis, split_axis=0, concat_axis=0, tiled=True)]
    reduce_sum x17 -> x0, other arithmetic: 4.64 us -> none  [the longest x16 4.57 us: greedy_step(): jnp.sum(jnp.maximum(similar_map - cover_now[:, None], 0.0), axis=0)]
    gather x2 -> x0, local copies, waits for them, and re-layouts: 2.86 us -> none  [the longest x1 2.2 us: per_device(): chosen_cols = jnp.take(similar_map, second_list, axis=1)]
  transfers between devices with their start and end apart: 2 -> 0, of which waited for: 2 -> 0; matrix products, arithmetic and copies ran while one was open for 5% -> 0% of each run, Pallas kernels for 0% -> 0%
where the time goes in v1:
time: 59.4 us; the launch traced here: 59.3 us
  Pallas kernels  54.9 us (92%)
  local copies, waits for them, and re-layouts  2.46 us (4%)
  other arithmetic  1.26 us (2%)
  between operations  0.64 us (1%)
    pallas_call x1, Pallas kernels, per_device(): pl.pallas_call(kernel, out_shape=(jax.ShapeDtypeStruct((1, 128), F32), ja...  54.9 us
    unnamed x1, local copies, waits for them, and re-layouts  1.27 us
    pallas_call x1, other arithmetic, per_device(): pl.pallas_call(kernel, out_shape=(jax.ShapeDtypeStruct((1, 128), F32), ja...  1.26 us

profile of v1, /device:TPU:1, one launch (start us, length us, event | category | flops | bytes accessed | tf_op | source)
XLA Modules:
  0.0 59.3 jit_solution(13442408955804984839)
XLA Ops:
  0.6 54.9 %coreset.1 = (f32[1,128]{1,0:T(1,128)}, f32[1,1024]{1,0:T(1,128)}) custom-call(s32[1,8]{1,0:T(1,128)} %local_ref.1, s32[1,16]{1,0:T(1,128)} %second_ref.1, s32[16]{0:T(128)} %final_ref.1, bf16[128,8,4096]{2,1,0:T(8,128)(2,1)} %bitcast.3), custom_call_target="tpu_custom_call" | custom-call | tf_op jit(solution)/shard_map/coreset/pallas_call | solution.py:320
  55.6 0.5 broadcast.3
  56.1 1.3 %reduce.3 = f32[128]{0:T(128)S(1)} reduce(f32[1,128]{1,0:T(1,128)} %get-tuple-element.4, f32[]{:T(128)} %broadcast.3), dimensions={0}, to_apply=%get-tuple-element.4.reduce_sub_computation.3 | reduce | bytes 1028 | tf_op jit(solution)/shard_map/coreset/pallas_call | solution.py:320
  57.3 0.7 %reshape.14 = f32[8,16]{1,0:T(8,128)} reshape(f32[128]{0:T(128)S(1)} %reduce.3) | data formatting | bytes 1024 | tf_op jit(solution)/shard_map/reshape | solution.py:359
  58.0 1.3 %copy.7 = f32[1024]{0:T(1024)} copy(f32[1024]{0:T(1024)} %bitcast.5) | data formatting | bytes 8192
